TPU v7x, 256 devices: a whole 4x4x8 slice. The times are simulated.
256 devices in a mesh: blk: 64 (over x, z_lo, y, core), pix: 4 (over z_hi).
Axes of the slice: x: 4, y: 4, z: 8 (z_hi: 4, z_lo: 2; z = z_hi * 2 + z_lo), core: 2. Of those that a mesh axis runs over, the one named last changes fastest.
Arguments:
- particles: bfloat16 [32768, 16384], P('blk', 'pix'), may hold values from -10 to 10, as said below
- ctf: bfloat16 [32768, 16384], P('blk', 'pix'), may hold values from -1 to 1
- noise_var: float32 [16384], P('pix'), may hold values from 0.5 to 4
- projections: bfloat16 [1024, 16384], P('blk', 'pix'), may hold values from -3.1 to 3.1
- orient_class: int32 [1024], replicated, may hold values from 0 to 4
- class_prior: float32 [5], replicated, may hold values from -2 to 0
- counts: int32 [64], P('blk'), may hold values from 32 to 512, as said below
Outputs:
- class_field: float32 [1024, 16384], P('blk', 'pix')
- normalizer: float32 [32768], P('blk')
Inputs may be any that keep to these rules, and one draw needn't show every extreme that they name: `particles`: real values of particle images. Live slots of each index of blk are its first counts slots; some index of blk is full in every draw.
All inputs are finite; a program needn't handle non-finite values.
Results may differ from a plain program's by a relative error of at most 0.0066.
Values may be sent and summed in bfloat16 or wider, within the bound.
A program may use at most 128 MiB of HBM per device.

v0:
```python
import jax
import jax.numpy as jnp
from jax import lax
from jax.sharding import Mesh
from jax.sharding import PartitionSpec as P

CLASSES = 5
BLK = ("blk_0", "blk_1", "blk_2", "blk_3")


def cut_along(value, dim, devices):
    lengths = value.shape
    tiles = value.reshape(*lengths[:dim], devices, lengths[dim] // devices, *lengths[dim + 1 :])
    return jnp.moveaxis(tiles, dim, 0)


def summed_on_arrival(value, axis, dim):
    devices = lax.axis_size(axis)
    tiles = lax.all_to_all(cut_along(value, dim, devices), axis, 0, 0, tiled=True)
    return jnp.sum(tiles, axis=0)


def from_everyone(value, axis):
    copies = jnp.broadcast_to(value, (lax.axis_size(axis), *value.shape))
    return lax.all_to_all(copies, axis, split_axis=0, concat_axis=0, tiled=True)


def of_everyone(value, axis):
    return from_everyone(value, axis).max(axis=0)


def of_everyone_2(value, axis):
    everything = from_everyone(value, axis)
    return jnp.sum(everything, axis=0)


def joined_along(tiles, dim):
    lengths = list(tiles.shape[1:])
    lengths[dim] *= tiles.shape[0]
    return jnp.moveaxis(tiles, 0, dim).reshape(lengths)


def collect(value, axis, dim):
    return joined_along(from_everyone(value, axis), dim)


def sum_by_chip_2(value, chips, core, dim):
    sizes = (lax.axis_size(chips), lax.axis_size(core))
    tiles = cut_along(value, dim, sizes[0] * sizes[1])
    inside = tiles.shape[1:]
    tiles = tiles.reshape(*sizes, *inside).swapaxes(0, 1).reshape(-1, *inside)
    tiles = lax.psum_scatter(tiles, core, scatter_dimension=0, tiled=True)
    return lax.psum_scatter(tiles, chips, scatter_dimension=0, tiled=True)[0]


def body(particles, ctf, noise_var, projections, orient_class, class_prior, counts):
    inverse = 1.0 / noise_var
    ctf_wide = ctf.astype(jnp.float32)
    weighted = (particles.astype(jnp.float32) * ctf_wide * inverse[None, :]).astype(jnp.bfloat16)
    quadratic = (0.5 * ctf_wide * ctf_wide * inverse[None, :]).astype(jnp.bfloat16)
    member = orient_class[:, None] == jnp.arange(CLASSES, dtype=jnp.int32)[None, :]
    orient_prior = jnp.sum(jnp.where(member, class_prior[None, :], jnp.float32(0.0)), axis=1)
    slot_count = particles.shape[0]
    live_slot = jnp.arange(slot_count, dtype=jnp.int32) < counts[0]
    part_rows = lax.all_gather(projections, BLK, axis=0, tiled=True)
    rows_wide = part_rows.astype(jnp.float32)
    piece_square = (rows_wide * rows_wide).astype(jnp.bfloat16)
    cross_term = lax.dot_general(
        weighted, part_rows, (((1,), (1,)), ((), ())), preferred_element_type=jnp.float32
    )
    square_term = lax.dot_general(
        quadratic, piece_square, (((1,), (1,)), ((), ())), preferred_element_type=jnp.float32
    )
    partial_value = cross_term - square_term
    share_cols = partial_value.shape[1] // lax.axis_size("pix")
    scores = summed_on_arrival(partial_value, "pix", 1)
    column_start = lax.axis_index("pix") * share_cols
    logits = scores + lax.dynamic_slice_in_dim(orient_prior, column_start, share_cols, 0)[None, :]
    peak_score = of_everyone(jnp.max(logits, axis=1), "pix")
    exp_total = of_everyone_2(jnp.sum(jnp.exp(logits - peak_score[:, None]), axis=1), "pix")
    log_total = peak_score + jnp.log(exp_total)
    share_weights = jnp.where(
        live_slot[:, None], jnp.exp(logits - log_total[:, None]), jnp.float32(0.0)
    ).astype(jnp.bfloat16)
    weights = collect(share_weights, "pix", 1)
    normalizer = jnp.where(live_slot, log_total, jnp.float32(0.0))
    class_field = sum_by_chip_2(
        lax.dot_general(
            weights, weighted, (((0,), (0,)), ((), ())), preferred_element_type=jnp.float32
        ),
        ("blk_0", "blk_1", "blk_2"),
        "blk_3",
        0,
    )
    return (class_field, normalizer)


def solution(mesh):
    torus = Mesh(
        mesh.devices.reshape(4, 2, 4, 2, mesh.shape["pix"]),
        ("blk_0", "blk_1", "blk_2", "blk_3", "pix"),
    )
    in_specs = (P(BLK, "pix"), P(BLK, "pix"), P("pix"), P(BLK, "pix"), P(), P(), P(BLK))
    out_specs = (P(BLK, "pix"), P(BLK))
    return jax.shard_map(body, mesh=torus, in_specs=in_specs, out_specs=out_specs, check_vma=False)
```

profile of v0, /device:TPU:8, one launch (start us, length us, event | category | flops | bytes accessed | tf_op | source)
XLA Modules:
  0.0 478.7 jit_solution(2758263446378586578)
XLA Ops:
  7.2 0.7 all-gather.2.cloned.1.call-update
  7.9 0.7 broadcast_divide_fusion
  8.6 116.4 %all-gather.2.cloned.1.call-done = bf16[1024,4096]{1,0:T(8,128)(2,1)} async-done(((bf16[16,4096]{1,0:T(8,128)(2,1)}), bf16[1024,4096]{1,0:T(8,128)(2,1)}) %all-gather.2.cloned.1.call-update) | async-done | bytes 8388624 | tf_op jit(solution)/shard_map/all_gather | solution.py:65
  125.0 9.6 %fusion.13 = f32[512,1024]{1,0:T(8,128)S(1)} fusion(bf16[1024,4096]{1,0:T(8,128)(2,1)} %all-gather.2.cloned.1.call-done, bf16[512,4096]{1,0:T(8,128)(2,1)} %param.8, bf16[512,4096]{1,0:T(8,128)(2,1)} %param.7, f32[4096]{0:T(1024)S(1)} %broadcast_divide_fusion), kind=kOutput, calls=%fused_computation.14 | convolution fusion | flops 4305453056 | bytes 18890752 | tf_op jit(solution)/shard_map/dot_general | solution.py:68
  134.6 4.6 fusion.9
  139.2 1.6 copy.30
  140.7 6.6 %all-to-all-start = ((f32[4,512,256]{2,1,0:T(8,128)}), f32[4,512,256]{2,1,0:T(8,128)S(1)}, u32[]{:S(2)}, u32[]{:S(2)}) async-start(f32[4,512,256]{2,1,0:T(8,128)} %bitcast.29), calls=%async_computation | async-start | bytes 4194304 | tf_op jit(solution)/shard_map/all_to_all | solution.py:19
  147.5 51.0 %all-to-all-done = f32[4,512,256]{2,1,0:T(8,128)S(1)} async-done(((f32[4,512,256]{2,1,0:T(8,128)}), f32[4,512,256]{2,1,0:T(8,128)S(1)}, u32[]{:S(2)}, u32[]{:S(2)}) %all-to-all-start) | async-done | bytes 2097184 | tf_op jit(solution)/shard_map/all_to_all | solution.py:19
  198.5 0.2 reduce_sum.36
  198.7 0.2 add_reduce_fusion
  198.8 0.6 broadcast_in_dim.49
  199.4 3.2 all-to-all-start.1
  203.3 7.0 %all-to-all-done.1 = f32[4,1,512]{2,1,0:T(1,128)S(1)} async-done(((f32[4,1,512]{2,1,0:T(1,128)}), f32[4,1,512]{2,1,0:T(1,128)S(1)}, u32[]{:S(2)}, u32[]{:S(2)}) %all-to-all-start.1) | async-done | bytes 8224 | tf_op jit(solution)/shard_map/all_to_all | solution.py:25
  210.4 0.2 exponential_reduce_fusion
  210.6 0.6 broadcast_in_dim.50
  211.2 3.2 all-to-all-start.2
  214.6 7.6 %all-to-all-done.2 = f32[4,1,512]{2,1,0:T(1,128)S(1)} async-done(((f32[4,1,512]{2,1,0:T(1,128)}), f32[4,1,512]{2,1,0:T(1,128)S(1)}, u32[]{:S(2)}, u32[]{:S(2)}) %all-to-all-start.2) | async-done | bytes 8224 | tf_op jit(solution)/shard_map/all_to_all | solution.py:25
  222.2 0.6 broadcast_select_fusion
  222.8 0.2 select_convert_fusion
  223.3 24.0 %all_to_all.22 = bf16[4,512,256]{1,2,0:T(8,128)(2,1)S(1)} all-to-all(bf16[4,512,256]{1,2,0:T(8,128)(2,1)S(1)} %broadcast_in_dim.52), channel_id=1, replica_groups=mesh['blk_0'=4,'blk_1'=2,'blk_2'=4,'blk_3'=2,'pix'=4] {'pix'}, dimensions={0} | all-to-all | bytes 2097152 | tf_op jit(solution)/shard_map/all_to_all | solution.py:25
  247.3 7.0 %convolution_bitcast_fusion = f32[2,32,16,4096]{3,2,0,1:T(8,128)S(1)} fusion(bf16[32,2,16,512]{3,2,1,0:T(8,128)(2,1)S(1)} %bitcast.31, bf16[512,4096]{1,0:T(8,128)(2,1)} %param.8, bf16[512,4096]{1,0:T(8,128)(2,1)} %param.7, f32[4096]{0:T(1024)S(1)} %broadcast_divide_fusion), kind=kOutput, calls=%fused_computation.3 | convolution fusion | flops 4305453056 | bytes 26230784 | tf_op jit(solution)/shard_map/dot_general | solution.py:88
  254.4 6.0 %copy.23 = f32[2,32,16,4096]{3,2,1,0:T(8,128)} copy(f32[2,32,16,4096]{3,2,0,1:T(8,128)S(1)} %convolution_bitcast_fusion) | data formatting | bytes 33554432 | tf_op jit(solution)/shard_map/transpose | solution.py:51
  260.5 28.5 %reduce-scatter.3.cloned.1.call-done = f32[32,16,4096]{2,1,0:T(8,128)} async-done(((f32[64,16,4096]{2,1,0:T(8,128)}), f32[32,16,4096]{2,1,0:T(8,128)}) %reduce-scatter.3.cloned.1.call-update) | async-done | bytes 8388624 | tf_op jit(solution)/shard_map/reduce_scatter | solution.py:52
  289.0 183.1 %reduce-scatter.5.cloned.1.call-done = f32[1,16,4096]{2,1,0:T(8,128)} async-done(((f32[32,16,4096]{2,1,0:T(8,128)}), f32[1,16,4096]{2,1,0:T(8,128)}) %reduce-scatter.5.cloned.1.call-update) | async-done | bytes 262160 | tf_op jit(solution)/shard_map/reduce_scatter | solution.py:53
  (20 shorter events, 0.6 us)
Async XLA Ops:
  7.2 117.8 %all-gather.2.cloned.1.call-start = ((), (), s32[]{:S(2)}) async-start(), calls=%async_computation.6 | async-start | bytes 8519680 | tf_op jit(solution)/shard_map/all_gather | solution.py:65
  125.0 9.6 %copy-start.2 = (bf16[1024,4096]{1,0:T(8,128)(2,1)S(1)}, bf16[1024,4096]{1,0:T(8,128)(2,1)}, u32[]{:S(2)}) copy-start(bf16[1024,4096]{1,0:T(8,128)(2,1)} %all-gather.2.cloned.1.call-done) | copy-start | bytes 25165828
  125.0 9.6 %copy-start.3 = (bf16[512,4096]{1,0:T(8,128)(2,1)S(1)}, bf16[512,4096]{1,0:T(8,128)(2,1)}, u32[]{:S(2)}) copy-start(bf16[512,4096]{1,0:T(8,128)(2,1)} %param.8) | copy-start | bytes 12582916
  139.2 8.1 %copy-start = (s32[1024]{0:T(1024)S(1)}, s32[1024]{0:T(1024)}, u32[]{:S(2)}) copy-start(s32[1024]{0:T(1024)} %param.11) | copy-start | bytes 12292
  139.2 8.1 %copy-start.1 = (f32[5]{0:T(128)S(1)}, f32[5]{0:T(128)}, u32[]{:S(2)}) copy-start(f32[5]{0:T(128)} %param.12) | copy-start | bytes 64
  140.7 57.7 %all-to-all-start = ((f32[4,512,256]{2,1,0:T(8,128)}), f32[4,512,256]{2,1,0:T(8,128)S(1)}, u32[]{:S(2)}, u32[]{:S(2)}) async-start(f32[4,512,256]{2,1,0:T(8,128)} %bitcast.29), calls=%async_computation | async-start | bytes 4194304 | tf_op jit(solution)/shard_map/all_to_all | solution.py:19
  199.4 11.0 %all-to-all-start.1 = ((f32[4,1,512]{2,1,0:T(1,128)}), f32[4,1,512]{2,1,0:T(1,128)S(1)}, u32[]{:S(2)}, u32[]{:S(2)}) async-start(f32[4,1,512]{2,1,0:T(1,128)} %broadcast_in_dim.49), calls=%async_computation.1 | async-start | bytes 16384 | tf_op jit(solution)/shard_map/all_to_all | solution.py:25
  211.2 11.0 %all-to-all-start.2 = ((f32[4,1,512]{2,1,0:T(1,128)}), f32[4,1,512]{2,1,0:T(1,128)S(1)}, u32[]{:S(2)}, u32[]{:S(2)}) async-start(f32[4,1,512]{2,1,0:T(1,128)} %broadcast_in_dim.50), calls=%async_computation.2 | async-start | bytes 16384 | tf_op jit(solution)/shard_map/all_to_all | solution.py:25
  214.5 74.5 %reduce-scatter.3.cloned.1.call-start = ((), (), s32[]{:S(2)}) async-start(), calls=%async_computation.7 | async-start | bytes 25165824 | tf_op jit(solution)/shard_map/reduce_scatter | solution.py:52
  260.4 211.7 %reduce-scatter.5.cloned.1.call-start = ((), (), s32[]{:S(2)}) async-start(), calls=%async_computation.8 | async-start | bytes 8650752 | tf_op jit(solution)/shard_map/reduce_scatter | solution.py:53
Sparse Core Ops, SparseCore 0:
  9.8 115.1 all-gather.1
  260.5 28.4 reduce-scatter.2
  292.1 179.9 reduce-scatter.4
where the time goes:
time: 484 us; the launch traced here: 479 us
  waiting for transfers between devices  394 us (81%)
  blocking collectives  24 us (5%)
  matrix products  21.2 us (4%)
  between operations  14.5 us (3%)
  starting transfers between devices  13.2 us (3%)
  local copies, waits for them, and re-layouts  9.11 us (2%)
    reduce_scatter x1, waiting for transfers between devices, sum_by_chip_2(): return lax.psum_scatter(tiles, chips, scatter_dimension=0, tiled=True)[0]  183 us
    all_gather x1, waiting for transfers between devices, body(): part_rows = lax.all_gather(projections, BLK, axis=0, tiled=True)  116 us
    all_to_all x1, waiting for transfers between devices, summed_on_arrival(): lax.all_to_all(cut_along(value, dim, devices), axis, 0, 0, tiled=True)  51 us
    reduce_scatter x1, waiting for transfers between devices, sum_by_chip_2(): tiles = lax.psum_scatter(tiles, core, scatter_dimension=0, tiled=True)  28.5 us
    all_to_all x1, blocking collectives, from_everyone(): return lax.all_to_all(copies, axis, split_axis=0, concat_axis=0, tiled=True)  24 us
    all_to_all x2, waiting for transfers between devices, from_everyone(): return lax.all_to_all(copies, axis, split_axis=0, concat_axis=0, tiled=True)  14.7 us
  transfers between devices with their start and end apart: 6, of which 6 were waited for; matrix products, arithmetic and copies ran while one was open for 0% of the time, Pallas kernels for 0%

commit v1 on v0

v1 whole, which is shorter than its diff:
```python
import jax
import jax.numpy as jnp
from jax import lax
from jax.experimental import pallas as pl
from jax.experimental.pallas import tpu as pltpu
from jax.sharding import Mesh
from jax.sharding import PartitionSpec as P

CLASSES = 5
BLK = ("blk_0", "blk_1", "blk_2", "blk_3")
MESH = pl.DeviceIdType.MESH
F32 = jnp.float32
BF16 = jnp.bfloat16
NSEM = 160


def kernel(
    part_hbm, ctf_hbm, nv_ref, own_ref, oc_ref, cp_ref, cnt_ref,
    out_ref, norm_ref,
    wgt, quad, proj, sq, pscore, rq, logit, stats, wts,
    cown, cpart, drecv, fsend, frecv, sbuf, ssend, srecv, zsend, zrecv,
    load_sem, send_sem, agr_sem, rq_sem, st_sem, w_sem, d_sem, f_sem, s_sem, z_sem,
):
    x = lax.axis_index("blk_0")
    z = lax.axis_index("blk_1")
    y = lax.axis_index("blk_2")
    c = lax.axis_index("blk_3")
    q = lax.axis_index("pix")
    npart, npix = part_hbm.shape

    def shifted(a, b):
        nx = lax.rem(x + a * (1 - c) + b * c, 4)
        ny = lax.rem(y + a * c + b * (1 - c), 4)
        return (nx, z, ny, c, q)

    fp, fm, sp, sm = shifted(1, 0), shifted(3, 0), shifted(0, 1), shifted(0, 3)
    zn = (x, 1 - z, y, c, q)
    pn = (x, z, y, 1 - c, q)
    qp, qm, q2 = ((x, z, y, c, lax.rem(q + k, 4)) for k in (1, 3, 2))
    peers = (fp, fm, sp, sm, zn, pn, qp, qm, q2)

    sends = []

    def send(src, dst, rsem, dev):
        copy = pltpu.make_async_remote_copy(
            src_ref=src, dst_ref=dst, send_sem=send_sem.at[len(sends)], recv_sem=rsem,
            device_id=dev, device_id_type=MESH,
        )
        copy.start()
        sends.append(copy)

    def arrived(dst, rsem):
        pltpu.make_async_remote_copy(
            src_ref=dst, dst_ref=dst, send_sem=send_sem.at[0], recv_sem=rsem,
            device_id=pn, device_id_type=MESH,
        ).wait_recv()

    pieces = 4
    rows = npart // pieces
    loads = []
    for i in range(pieces):
        for k, (src, dst) in enumerate(((part_hbm, wgt), (ctf_hbm, quad))):
            cp = pltpu.make_async_copy(
                src.at[pl.ds(i * rows, rows)], dst.at[pl.ds(i * rows, rows)], load_sem.at[2 * i + k]
            )
            cp.start()
            loads.append(cp)

    barrier = pltpu.get_barrier_semaphore()
    for dev in peers:
        pl.semaphore_signal(barrier, inc=1, device_id=dev, device_id_type=MESH)
    pl.semaphore_wait(barrier, len(peers))

    def slab_no(f, s, k, dz):
        return (((f % 4) * 4 + s % 4) * 2 + k) * 2 + dz

    def slab(f, s, k, dz):
        return proj.at[pl.ds(slab_no(f, s, k, dz) * 16, 16)]

    def ag(src, f, s, k, dz, dev):
        send(src, slab(f, s, k, dz), agr_sem.at[slab_no(f, s, k, dz)], dev)

    def ag_wait(f, s, k, dz):
        arrived(slab(f, s, k, dz), agr_sem.at[slab_no(f, s, k, dz)])

    def to_partner(f, s, dz):
        ag(slab(f, s, 0, dz), f, s, 1, dz, pn)

    def to_second(f, dz):
        ag(slab(f, 0, 0, dz), f, 3, 0, dz, sp)
        ag(slab(f, 0, 0, dz), f, 1, 0, dz, sm)

    ag(own_ref, 0, 0, 0, 1, zn)
    ag(own_ref, 3, 0, 0, 0, fp)
    ag(own_ref, 1, 0, 0, 0, fm)
    ag(own_ref, 0, 3, 0, 0, sp)
    ag(own_ref, 0, 1, 0, 0, sm)
    ag(own_ref, 0, 0, 1, 0, pn)
    slab(0, 0, 0, 0)[...] = own_ref[...]

    inverse = 1.0 / nv_ref[...]

    def prepare(i):
        loads[2 * i].wait()
        loads[2 * i + 1].wait()

        @pl.loop(0, rows // 16)
        def _(r):
            at = pl.ds(pl.multiple_of(i * rows + r * 16, 16), 16)
            for h in range(npix // 1024):
                cols = pl.ds(h * 1024, 1024)
                inv = inverse[:, h * 1024 : (h + 1) * 1024]
                wide = quad[at, cols].astype(F32)
                wgt[at, cols] = (wgt[at, cols].astype(F32) * wide * inv).astype(BF16)
                quad[at, cols] = (0.5 * wide * wide * inv).astype(BF16)

    prepare(0)
    prepare(1)
    ag_wait(3, 0, 0, 0)
    ag(slab(3, 0, 0, 0), 2, 0, 0, 0, fp)
    to_partner(3, 0, 0)
    ag_wait(1, 0, 0, 0)
    to_partner(1, 0, 0)
    ag_wait(0, 3, 0, 0)
    ag(slab(0, 3, 0, 0), 0, 2, 0, 0, sp)
    to_partner(0, 3, 0)
    ag_wait(0, 1, 0, 0)
    to_partner(0, 1, 0)
    ag_wait(0, 0, 0, 1)
    ag(slab(0, 0, 0, 1), 3, 0, 0, 1, fp)
    ag(slab(0, 0, 0, 1), 1, 0, 0, 1, fm)
    to_second(0, 1)
    to_second(3, 0)
    to_second(1, 0)
    to_partner(0, 0, 1)
    prepare(2)
    prepare(3)
    ag_wait(0, 3, 0, 1)
    to_partner(0, 3, 1)
    ag_wait(0, 1, 0, 1)
    ag(slab(0, 1, 0, 1), 0, 2, 0, 1, sm)
    to_partner(0, 1, 1)
    ag_wait(1, 0, 0, 1)
    ag(slab(1, 0, 0, 1), 2, 0, 0, 1, fm)
    to_second(1, 1)
    to_partner(1, 0, 1)
    ag_wait(3, 0, 0, 1)
    to_second(3, 1)
    to_partner(3, 0, 1)
    ag_wait(2, 0, 0, 0)
    to_second(2, 0)
    to_partner(2, 0, 0)
    for dz in (0, 1):
        ag_wait(0, 2, 0, dz)
        to_partner(0, 2, dz)

    lane = lax.broadcasted_iota(jnp.int32, (1, 1024), 1)
    prior_row = jnp.zeros((1, 1024), F32)
    for k in range(CLASSES):
        prior_row = jnp.where(oc_ref[...] == k, cp_ref[k], prior_row)
    row = lax.broadcasted_iota(jnp.int32, (256, 1), 0)
    rf, rk, rz, rr = row // 64, (row // 32) % 2, (row // 16) % 2, row % 16
    co = (c + rk) % 2
    ox = (x + rf * (1 - co) + q * co) % 4
    oy = (y + rf * co + q * (1 - co)) % 4
    oz = (z + rz) % 2
    number = (((ox * 2 + oz) * 4 + oy) * 2 + co) * 16 + rr
    prior = jnp.sum(jnp.where(number == lane, prior_row, 0.0), axis=1, keepdims=True)

    nt = (((1,), (1,)), ((), ()))

    def scores(f):
        group = proj.at[pl.ds(f * 256, 256)]

        @pl.loop(0, 16)
        def _(r):
            at = pl.ds(pl.multiple_of(r * 16, 16), 16)
            wide = group[at, :].astype(F32)
            sq[at, :] = (wide * wide).astype(BF16)

        for h in range(npart // 256):
            some = pl.ds(h * 256, 256)
            cross = lax.dot_general(group[...], wgt[some, :], nt, preferred_element_type=F32)
            square = lax.dot_general(sq[...], quad[some, :], nt, preferred_element_type=F32)
            pscore[pl.ds(f * 256, 256), some] = cross - square

    def prow(f, k, half):
        return pl.ds(pl.multiple_of(f * 256 + lax.rem(q + k, 4) * 64 + half * 32, 32), 32)

    def rq_send(f, k, half, slot, dev):
        send(pscore.at[prow(f, k, half)], rq.at[f * 6 + slot], rq_sem.at[f * 6 + slot], dev)

    def rq_wait(f, slot):
        arrived(rq.at[f * 6 + slot], rq_sem.at[f * 6 + slot])

    def rq_first(f):
        rq_send(f, 2, 0, 0, qp)
        rq_send(f, 2, 1, 1, qm)
        rq_send(f, 1, 1, 2, qp)
        rq_send(f, 3, 0, 3, qm)

    def rq_second(f):
        rq_wait(f, 0)
        pscore[prow(f, 1, 0), :] += rq[f * 6]
        rq_send(f, 1, 0, 4, qp)
        rq_wait(f, 1)
        pscore[prow(f, 3, 1), :] += rq[f * 6 + 1]
        rq_send(f, 3, 1, 5, qm)

    def rq_third(f):
        for slot in (2, 3, 4, 5):
            rq_wait(f, slot)
        logit[pl.ds(f * 64, 32), :] = (
            pscore[prow(f, 0, 0), :] + rq[f * 6 + 3] + rq[f * 6 + 4] + prior[f * 64 : f * 64 + 32]
        )
        logit[pl.ds(f * 64 + 32, 32), :] = (
            pscore[prow(f, 0, 1), :] + rq[f * 6 + 2] + rq[f * 6 + 5] + prior[f * 64 + 32 : f * 64 + 64]
        )

    def rest_of_group(f):
        for dz in (0, 1):
            if f == 2 and dz == 1:
                ag_wait(2, 0, 0, 1)
                to_second(2, 1)
                to_partner(2, 0, 1)
            ag_wait(f, 3, 0, dz)
            if dz == 0:
                ag(slab(f, 3, 0, 0), f, 2, 0, 0, sp)
            to_partner(f, 3, dz)
            ag_wait(f, 1, 0, dz)
            if dz == 1:
                ag(slab(f, 1, 0, 1), f, 2, 0, 1, sm)
            to_partner(f, 1, dz)

    def end_of_group(f):
        for dz in (0, 1):
            ag_wait(f, 2, 0, dz)
            to_partner(f, 2, dz)

    def partners_group(f):
        for s in range(4):
            for dz in (0, 1):
                ag_wait(f, s, 1, dz)

    partners_group(0)
    scores(0)
    rq_first(0)
    ag_wait(2, 0, 0, 1)
    to_second(2, 1)
    to_partner(2, 0, 1)

    def group(f):
        for dz in (0, 1):
            ag_wait(f, 3, 0, dz)
            if dz == 0:
                ag(slab(f, 3, 0, 0), f, 2, 0, 0, sp)
            to_partner(f, 3, dz)
            ag_wait(f, 1, 0, dz)
            if dz == 1:
                ag(slab(f, 1, 0, 1), f, 2, 0, 1, sm)
            to_partner(f, 1, dz)
        end_of_group(f)
        partners_group(f)

    order = (0, 1, 3, 2)
    for before, f in zip(order, order[1:]):
        group(f)
        scores(f)
        rq_first(f)
        rq_second(before)
    for f in order[:-1]:
        rq_third(f)
    rq_second(2)
    rq_third(2)

    peak = jnp.max(logit[...], axis=0, keepdims=True)
    total = jnp.sum(jnp.exp(logit[...] - peak), axis=0, keepdims=True)
    stats[0, 0:1, :] = peak
    stats[0, 1:2, :] = total
    for k, dev in ((3, qp), (1, qm), (2, q2)):
        send(stats.at[0], stats.at[k], st_sem.at[k], dev)
    for k in (1, 3, 2):
        arrived(stats.at[k], st_sem.at[k])
    top = peak
    for k in (1, 2, 3):
        top = jnp.maximum(top, stats[k, 0:1, :])
    full = total * jnp.exp(peak - top)
    for k in (1, 2, 3):
        full += stats[k, 1:2, :] * jnp.exp(stats[k, 0:1, :] - top)
    lse = top + jnp.log(full)
    live = lax.broadcasted_iota(jnp.int32, (1, npart), 1) < cnt_ref[0]
    norm_ref[...] = jnp.where(live, lse, 0.0)
    wts[0] = jnp.where(live, jnp.exp(logit[...] - lse), 0.0).astype(BF16)

    def w_half(k, half):
        return wts.at[k, pl.ds(half * 128, 128)]

    def w_send(a, b, half, dev):
        send(w_half(a, half), w_half(b, half), w_sem.at[b * 2 + half], dev)

    def w_wait(k, half):
        arrived(w_half(k, half), w_sem.at[k * 2 + half])

    w_send(0, 3, 0, qp)
    w_send(0, 1, 1, qm)
    w_send(0, 3, 1, qp)
    w_send(0, 1, 0, qm)

    def classes(k):
        @pl.loop(0, npix // 512)
        def _(h):
            cols = pl.ds(pl.multiple_of(h * 512, 512), 512)
            res = jnp.dot(wts[k], wgt[:, cols], preferred_element_type=F32)
            for f in range(4):
                cown[k, pl.ds(f * 32, 32), cols] = res[f * 64 : f * 64 + 32]
                cpart[k, pl.ds(f * 32, 32), cols] = res[f * 64 + 32 : f * 64 + 64].astype(BF16)

        send(cpart.at[k], drecv.at[k], d_sem.at[k], pn)

    def add_partner(k):
        arrived(drecv.at[k], d_sem.at[k])

        @pl.loop(0, npix // 512)
        def _(h):
            cols = pl.ds(pl.multiple_of(h * 512, 512), 512)
            cown[k, :, cols] += drecv[k, :, cols].astype(F32)

    def ring_first(src, out, inc, sem, dp, dm):
        for n, (j, dz, dev) in enumerate(((2, 0, dp), (2, 1, dm), (1, 1, dp), (3, 0, dm))):
            out[n] = src(j, dz)[...].astype(BF16)
            send(out.at[n], inc.at[n], sem.at[n], dev)

    def ring_second(src, out, inc, sem, dp, dm):
        for n, (j, dz, dev) in enumerate(((1, 0, dp), (3, 1, dm))):
            arrived(inc.at[n], sem.at[n])
            out[4 + n] = (src(j, dz)[...] + inc[n].astype(F32)).astype(BF16)
            send(out.at[4 + n], inc.at[4 + n], sem.at[4 + n], dev)

    def ring_third(src, inc, sem):
        for n in (2, 3, 4, 5):
            arrived(inc.at[n], sem.at[n])
        first = src(0, 0)[...] + inc[3].astype(F32) + inc[4].astype(F32)
        second = src(0, 1)[...] + inc[2].astype(F32) + inc[5].astype(F32)
        return first, second

    def f_args(k):
        return (
            lambda j, dz: cown.at[k, pl.ds(j * 32 + dz * 16, 16)],
            fsend.at[pl.ds(k * 6, 6)], frecv.at[pl.ds(k * 6, 6)], f_sem.at[pl.ds(k * 6, 6)], fp, fm,
        )

    def f_third(k):
        src, _, inc, sem, _, _ = f_args(k)
        first, second = ring_third(src, inc, sem)
        at = lax.rem(q + k, 4)
        sbuf[at, 0] = first
        sbuf[at, 1] = second

    classes(0)
    w_wait(3, 0)
    w_send(3, 2, 0, qp)
    w_wait(1, 1)
    w_send(1, 2, 1, qm)
    add_partner(0)
    ring_first(*f_args(0))
    w_wait(3, 1)
    classes(3)
    ring_second(*f_args(0))
    w_wait(1, 0)
    classes(1)
    add_partner(3)
    ring_first(*f_args(3))
    f_third(0)
    add_partner(1)
    ring_first(*f_args(1))
    ring_second(*f_args(3))
    w_wait(2, 0)
    w_wait(2, 1)
    classes(2)
    ring_second(*f_args(1))
    f_third(3)
    add_partner(2)
    ring_first(*f_args(2))
    f_third(1)
    ring_second(*f_args(2))
    f_third(2)

    s_args = (lambda j, dz: sbuf.at[j, dz], ssend, srecv, s_sem, sp, sm)
    ring_first(*s_args)
    ring_second(*s_args)
    mine, other = ring_third(s_args[0], srecv, s_sem)
    zsend[...] = other.astype(BF16)
    send(zsend, zrecv, z_sem, zn)
    out_ref[...] = mine
    arrived(zrecv, z_sem)
    out_ref[...] += zrecv[...].astype(F32)

    for copy in sends:
        copy.wait_send()


def body(particles, ctf, noise_var, projections, orient_class, class_prior, counts):
    npart, npix = particles.shape
    vmem = pl.BlockSpec(memory_space=pltpu.VMEM)
    smem = pl.BlockSpec(memory_space=pltpu.SMEM)
    hbm = pl.BlockSpec(memory_space=pl.ANY)
    dma = pltpu.SemaphoreType.DMA
    out, norm = pl.pallas_call(
        kernel,
        out_shape=(jax.ShapeDtypeStruct((16, npix), F32), jax.ShapeDtypeStruct((1, npart), F32)),
        in_specs=[hbm, hbm, vmem, vmem, vmem, smem, smem],
        out_specs=(vmem, vmem),
        scratch_shapes=[
            pltpu.VMEM((npart, npix), BF16),
            pltpu.VMEM((npart, npix), BF16),
            pltpu.VMEM((1024, npix), BF16),
            pltpu.VMEM((256, npix), BF16),
            pltpu.VMEM((1024, npart), F32),
            pltpu.VMEM((24, 32, npart), F32),
            pltpu.VMEM((256, npart), F32),
            pltpu.VMEM((4, 8, npart), F32),
            pltpu.VMEM((4, 256, npart), BF16),
            pltpu.VMEM((4, 128, npix), F32),
            pltpu.VMEM((4, 128, npix), BF16),
            pltpu.VMEM((4, 128, npix), BF16),
            pltpu.VMEM((24, 16, npix), BF16),
            pltpu.VMEM((24, 16, npix), BF16),
            pltpu.VMEM((4, 2, 16, npix), F32),
            pltpu.VMEM((6, 16, npix), BF16),
            pltpu.VMEM((6, 16, npix), BF16),
            pltpu.VMEM((16, npix), BF16),
            pltpu.VMEM((16, npix), BF16),
            dma((8,)), dma((NSEM,)), dma((64,)), dma((24,)), dma((4,)), dma((8,)), dma((4,)),
            dma((24,)), dma((6,)), dma,
        ],
        compiler_params=pltpu.CompilerParams(
            collective_id=0, has_side_effects=True, vmem_limit_bytes=64 * 1024 * 1024 - 128 * 1024
        ),
    )(particles, ctf, noise_var.reshape(1, npix), projections, orient_class.reshape(1, 1024), class_prior, counts)
    return out, norm.reshape(npart)


def solution(mesh):
    torus = Mesh(
        mesh.devices.reshape(4, 2, 4, 2, mesh.shape["pix"]),
        ("blk_0", "blk_1", "blk_2", "blk_3", "pix"),
    )
    in_specs = (P(BLK, "pix"), P(BLK, "pix"), P("pix"), P(BLK, "pix"), P(), P(), P(BLK))
    out_specs = (P(BLK, "pix"), P(BLK))
    return jax.shard_map(body, mesh=torus, in_specs=in_specs, out_specs=out_specs, check_vma=False)
```

time: 484 us -> 142 us (0.29)
  waiting for transfers between devices: 394 us -> 0 us
  Pallas kernels: 0 us -> 137 us
  blocking collectives: 24 us -> 0 us
  matrix products: 21.2 us -> 0 us
  between operations: 14.5 us -> 1.29 us
  starting transfers between devices: 13.2 us -> 0 us
  local copies, waits for them, and re-layouts: 9.11 us -> 2.92 us
    reduce_scatter x2 -> x0, waiting for transfers between devices: 212 us -> none  [the longest x1 183 us: sum_by_chip_2(): return lax.psum_scatter(tiles, chips, scatter_dimension=0, tiled=True)[0]]
    pallas_call x0 -> x1, Pallas kernels: none -> 137 us  [body(): pl.pallas_call(kernel, out_shape=(jax.ShapeDtypeStruct((16, npix), F32),...]
    all_gather x1 -> x0, waiting for transfers between devices: 116 us -> none  [body(): part_rows = lax.all_gather(projections, BLK, axis=0, tiled=True)]
    all_to_all x3 -> x0, waiting for transfers between devices: 65.7 us -> none  [the longest x1 51 us: summed_on_arrival(): lax.all_to_all(cut_along(value, dim, devices), axis, 0, 0, tiled=True)]
    all_to_all x1 -> x0, blocking collectives: 24 us -> none  [from_everyone(): return lax.all_to_all(copies, axis, split_axis=0, concat_axis=0, tiled=True)]
    dot_general x3 -> x0, matrix products: 21.2 us -> none  [the longest x1 9.56 us: body(): lax.dot_general(weighted, part_rows, (((1,), (1,)), ((), ())), preferred_...]
    all_to_all x3 -> x0, starting transfers between devices: 13.1 us -> none  [the longest x1 6.56 us: summed_on_arrival(): lax.all_to_all(cut_along(value, dim, devices), axis, 0, 0, tiled=True)]
    transpose x1 -> x0, local copies, waits for them, and re-layouts: 6.03 us -> none  [sum_by_chip_2(): tiles = tiles.reshape(*sizes, *inside).swapaxes(0, 1).reshape(-1, *inside)]
  transfers between devices with their start and end apart: 6 -> 0, of which waited for: 6 -> 0; matrix products, arithmetic and copies ran while one was open for 0% -> 0% of each run, Pallas kernels for 0% -> 0%
where the time goes in v1:
time: 142 us; the launch traced here: 141 us
  Pallas kernels  137 us (96%)
  local copies, waits for them, and re-layouts  2.92 us (2%)
    pallas_call x1, Pallas kernels, body(): pl.pallas_call(kernel, out_shape=(jax.ShapeDtypeStruct((16, npix), F32),...  137 us
    unnamed x2, local copies, waits for them, and re-layouts  2.92 us

profile of v1, /device:TPU:8, one launch (start us, length us, event | category | flops | bytes accessed | tf_op | source)
XLA Modules:
  0.0 141.4 jit_solution(7005112397609637376)
XLA Ops:
  1.3 137.2 %shard_map.86 = (f32[16,4096]{1,0:T(8,128)}, f32[1,512]{1,0:T(1,128)}) custom-call(bf16[512,4096]{1,0:T(8,128)(2,1)} %part_hbm.1, bf16[512,4096]{1,0:T(8,128)(2,1)} %ctf_hbm.1, f32[1,4096]{1,0:T(1,128)} %bitcast.3, bf16[16,4096]{1,0:T(8,128)(2,1)} %own_ref.1, s32[1,1024]{1,0:T(1,128)} %bitcast.4, f32[5]{0:T(128)} %cp_ref.1, s32[1]{0:T(128)S(6)} %copy.11.cnt_ref), custom_call_target="tpu_custom_call" | custom-call | tf_op jit(solution)/shard_map/pallas_call | solution.py:408
  138.5 1.7 %copy.12 = f32[16,4096]{1,0:T(8,128)} copy(f32[16,4096]{1,0:T(8,128)} %get-tuple-element.8) | data formatting | bytes 524288
  140.1 1.2 copy.13

commit v2 on v0

v2 whole, which is shorter than its diff:
```python
import jax
import jax.numpy as jnp
from jax import lax
from jax.experimental import pallas as pl
from jax.experimental.pallas import tpu as pltpu
from jax.sharding import Mesh
from jax.sharding import PartitionSpec as P

CLASSES = 5
BLK = ("blk_0", "blk_1", "blk_2", "blk_3")
MESH = pl.DeviceIdType.MESH
F32 = jnp.float32
BF16 = jnp.bfloat16
NSEM = 320
CHUNKS = (1, 2, 2, 1)
MAXCH = 4
PLACE = (3, 1, 0, 2)


def kernel(
    part_hbm, ctf_hbm, nv_hbm, own_hbm, oc_hbm, cp_ref, cnt_ref,
    out_ref, norm_ref,
    nv_ref, own_ref, oc_ref,
    wgt, ctf, wgt_t, quad_t, proj, sq, pscore, rq, logit, stats, wts,
    cown, cpart, drecv, fsend, frecv, ssend, srecv, szrecv, szown, zsend, zrecv, wn, scale,
    load_sem, send_sem, agr_sem, rq_sem, st_sem, w_sem, d_sem, f_sem, ss_sem, s_sem, sz_sem, z_sem,
):
    x = lax.axis_index("blk_0")
    z = lax.axis_index("blk_1")
    y = lax.axis_index("blk_2")
    c = lax.axis_index("blk_3")
    q = lax.axis_index("pix")
    npart, npix = part_hbm.shape

    def shifted(a, b):
        nx = lax.rem(x + a * (1 - c) + b * c, 4)
        ny = lax.rem(y + a * c + b * (1 - c), 4)
        return (nx, z, ny, c, q)

    fp, fm, sp, sm = shifted(1, 0), shifted(3, 0), shifted(0, 1), shifted(0, 3)
    zn = (x, 1 - z, y, c, q)
    pn = (x, z, y, 1 - c, q)
    qp, qm, q2 = ((x, z, y, c, lax.rem(q + k, 4)) for k in (1, 3, 2))
    far = [shifted(0, k) for k in (1, 2, 3)]
    peers = (fp, fm, sp, sm, zn, pn, qp, qm, q2, far[1], *((a, 1 - b, *rest) for a, b, *rest in far))

    sends = []

    def send(src, dst, rsem, dev):
        copy = pltpu.make_async_remote_copy(
            src_ref=src, dst_ref=dst, send_sem=send_sem.at[len(sends)], recv_sem=rsem,
            device_id=dev, device_id_type=MESH,
        )
        copy.start()
        sends.append(copy)

    def arrived(dst, rsem):
        pltpu.make_async_remote_copy(
            src_ref=dst, dst_ref=dst, send_sem=send_sem.at[0], recv_sem=rsem,
            device_id=pn, device_id_type=MESH,
        ).wait_recv()

    barrier = pltpu.get_barrier_semaphore()
    for dev in peers:
        pl.semaphore_signal(barrier, inc=1, device_id=dev, device_id_type=MESH)

    small = []
    for i, (src, dst) in enumerate(((own_hbm, own_ref), (nv_hbm, nv_ref), (oc_hbm, oc_ref))):
        cp = pltpu.make_async_copy(src, dst, load_sem.at[8 + i])
        cp.start()
        small.append(cp)
    pieces = 4
    rows = npart // pieces
    loads = []
    for i in range(pieces):
        for k, (src, dst) in enumerate(((part_hbm, wgt), (ctf_hbm, ctf))):
            cp = pltpu.make_async_copy(
                src.at[pl.ds(i * rows, rows)], dst.at[pl.ds(i * rows, rows)], load_sem.at[2 * i + k]
            )
            cp.start()
            loads.append(cp)

    small[0].wait()
    pl.semaphore_wait(barrier, len(peers))

    def slab_no(f, s, k, dz):
        return (((f % 4) * 2 + dz) * 4 + s % 4) * 2 + k

    def slab(f, s, k, dz):
        return proj.at[pl.ds(slab_no(f, s, k, dz) * 16, 16)]

    def ag(src, f, s, k, dz, dev):
        send(src, slab(f, s, k, dz), agr_sem.at[slab_no(f, s, k, dz)], dev)

    def ag_wait(f, s, k, dz):
        arrived(slab(f, s, k, dz), agr_sem.at[slab_no(f, s, k, dz)])

    def to_partner(f, s, dz):
        ag(slab(f, s, 0, dz), f, s, 1, dz, pn)

    def to_second(f, dz):
        ag(slab(f, 0, 0, dz), f, 3, 0, dz, sp)
        ag(slab(f, 0, 0, dz), f, 1, 0, dz, sm)

    ag(own_ref, 0, 0, 0, 1, zn)
    ag(own_ref, 1, 0, 0, 0, fm)
    ag(own_ref, 0, 3, 0, 0, sp)
    slab(0, 0, 0, 0)[...] = own_ref[...]

    small[1].wait()
    small[2].wait()
    def prepare(i):
        loads[2 * i].wait()
        loads[2 * i + 1].wait()
        at = pl.ds(i * rows, rows)

        @pl.loop(0, npix // 256)
        def _(h):
            cols = pl.ds(pl.multiple_of(h * 256, 256), 256)
            inv = 1.0 / nv_ref[:, cols]
            wide = ctf[at, cols].astype(F32)
            weighted = (wgt[at, cols].astype(F32) * wide * inv).astype(BF16)
            wgt[at, cols] = weighted
            wgt_t[cols, at] = weighted.T
            quad_t[cols, at] = (0.5 * wide * wide * inv).astype(BF16).T

    lane = lax.broadcasted_iota(jnp.int32, (1, 1024), 1)
    prior_row = jnp.zeros((1, 1024), F32)
    for k in range(CLASSES):
        prior_row = jnp.where(oc_ref[...] == k, cp_ref[k], prior_row)
    row = lax.broadcasted_iota(jnp.int32, (256, 1), 0)
    rp, rz, rk, rr = row // 64, (row // 32) % 2, (row // 16) % 2, row % 16
    rf = jnp.where(rp == 0, 2, jnp.where(rp == 1, 1, jnp.where(rp == 2, 3, 0)))
    co = (c + rk) % 2
    ox = (x + rf * (1 - co) + q * co) % 4
    oy = (y + rf * co + q * (1 - co)) % 4
    oz = (z + rz) % 2
    number = (((ox * 2 + oz) * 4 + oy) * 2 + co) * 16 + rr
    prior = jnp.sum(jnp.where(number == lane, prior_row, 0.0), axis=1, keepdims=True)

    def scores(g):
        group = proj.at[pl.ds(g * 128, 128)]
        wide = group[...].astype(F32)
        sq[...] = (wide * wide).astype(BF16)
        for h in range(npart // 256):
            some = pl.ds(h * 256, 256)
            cross = jnp.dot(group[...], wgt_t[:, some], preferred_element_type=F32)
            square = jnp.dot(sq[...], quad_t[:, some], preferred_element_type=F32)
            pscore[pl.ds(g * 128, 128), some] = cross - square

    def prow(g, k, half):
        return pl.ds(pl.multiple_of(g * 128 + lax.rem(q + k, 4) * 32 + half * 16, 16), 16)

    def rq_send(g, k, half, slot, dev):
        send(pscore.at[prow(g, k, half)], rq.at[g * 6 + slot], rq_sem.at[g * 6 + slot], dev)

    def rq_wait(g, slot):
        arrived(rq.at[g * 6 + slot], rq_sem.at[g * 6 + slot])

    def rq_far(g):
        rq_send(g, 2, 0, 0, qp)
        rq_send(g, 2, 1, 1, qm)

    def rq_near(g):
        rq_send(g, 1, 1, 2, qp)
        rq_send(g, 3, 0, 3, qm)

    def rq_second(g, way):
        rq_wait(g, way)
        at = prow(g, 1 + 2 * way, way)
        pscore[at, :] += rq[g * 6 + way]
        rq_send(g, 1 + 2 * way, way, 4 + way, (qp, qm)[way])

    def rq_third(g):
        for slot in (2, 3, 4, 5):
            rq_wait(g, slot)
        at = (PLACE[g // 2] * 2 + g % 2) * 32
        logit[pl.ds(at, 16), :] = (
            pscore[prow(g, 0, 0), :] + rq[g * 6 + 3] + rq[g * 6 + 4] + prior[at : at + 16]
        )
        logit[pl.ds(at + 16, 16), :] = (
            pscore[prow(g, 0, 1), :] + rq[g * 6 + 2] + rq[g * 6 + 5] + prior[at + 16 : at + 32]
        )

    def got(f, s, dz):
        ag_wait(f, s, 0, dz)
        if s == 3 and dz == 0:
            ag(slab(f, 3, 0, 0), f, 2, 0, 0, sp)
        if s == 1 and dz == 1:
            ag(slab(f, 1, 0, 1), f, 2, 0, 1, sm)
        if s == 0 and f == 3 and dz == 0:
            ag(slab(3, 0, 0, 0), 2, 0, 0, 0, fp)
        if s == 0 and f == 1 and dz == 1:
            ag(slab(1, 0, 0, 1), 2, 0, 0, 1, fm)
        to_partner(f, s, dz)

    def partners(f, dz):
        for s in range(4):
            ag_wait(f, s, 1, dz)

    live = lax.broadcasted_iota(jnp.int32, (1, npart), 1) < cnt_ref[0]

    def peak():
        most = jnp.max(logit[...], axis=0, keepdims=True)
        e = jnp.exp(logit[...] - most)
        stats[0, 0:1, :] = most
        stats[0, 1:2, :] = jnp.sum(e, axis=0, keepdims=True)
        wts[0] = e.astype(BF16)
        for k, dev in ((3, qp), (1, qm), (2, q2)):
            send(stats.at[0], stats.at[k], st_sem.at[k], dev)

    def softmax():
        for k in (1, 3, 2):
            arrived(stats.at[k], st_sem.at[k])
        peaks = [stats[k, 0:1, :] for k in range(4)]
        top = jnp.maximum(jnp.maximum(peaks[0], peaks[1]), jnp.maximum(peaks[2], peaks[3]))
        full = sum(stats[k, 1:2, :] * jnp.exp(peaks[k] - top) for k in range(4))
        lse = top + jnp.log(full)
        norm_ref[...] = jnp.where(live, lse, 0.0)
        for k in (1, 2, 3):
            scale[k, 0:1, :] = jnp.where(live, jnp.exp(peaks[k] - lse), 0.0)
        wn[0] = jnp.where(live, jnp.exp(logit[...] - lse), 0.0).astype(BF16)

    def w_piece(k, p):
        return wts.at[k, pl.ds(p * 64, 64)]

    def w_send(a, b, p, dev):
        send(w_piece(a, p), w_piece(b, p), w_sem.at[b * 4 + p], dev)

    def w_wait(k, p):
        arrived(w_piece(k, p), w_sem.at[k * 4 + p])
        if k == 3 and p % 2 == 0:
            w_send(3, 2, p, qp)
        if k == 1 and p % 2 == 1:
            w_send(1, 2, p, qm)

    def w_start():
        for p in range(4):
            w_send(0, 3, p, qp)
            w_send(0, 1, p, qm)

    def cols_of(h, n):
        return pl.ds(h * (npix // n), npix // n)

    def classes(k, part, h):
        n = CHUNKS[k]
        base = part * 64
        half = pl.ds(part * 128, 128)
        if k > 0 and h == 0:
            wn[k, half] = (wts[k, half].astype(F32) * scale[k, 0:1, :]).astype(BF16)
        for i in range(npix // n // 512):
            cols = pl.ds(h * (npix // n) + i * 512, 512)
            res = jnp.dot(wn[k, half], wgt[:, cols], preferred_element_type=F32)
            for g in range(4):
                cown[k, pl.ds(base + g * 16, 16), cols] = res[g * 32 : g * 32 + 16]
                cpart[k, pl.ds(base + g * 16, 16), cols] = res[g * 32 + 16 : g * 32 + 32].astype(BF16)
        at = (k, pl.ds(base, 64), cols_of(h, n))
        send(cpart.at[at], drecv.at[at], d_sem.at[(k * 2 + part) * MAXCH + h], pn)

    def own(k, j, dz, cols):
        return cown.at[k, pl.ds((PLACE[j] * 2 + dz) * 16, 16), cols]

    def ring_send(k, h, n, slot, value, dev):
        at = (k * 6 + slot, slice(None), cols_of(h, n))
        fsend[at] = value.astype(BF16)
        send(fsend.at[at], frecv.at[at], f_sem.at[(k * 6 + slot) * MAXCH + h], dev)

    def ring_wait(k, h, n, slot):
        at = (k * 6 + slot, slice(None), cols_of(h, n))
        arrived(frecv.at[at], f_sem.at[(k * 6 + slot) * MAXCH + h])
        return frecv[at].astype(F32)

    def first(k, part, h):
        n = CHUNKS[k]
        at = (k, pl.ds(part * 64, 64), cols_of(h, n))
        arrived(drecv.at[at], d_sem.at[(k * 2 + part) * MAXCH + h])

        def both(j, dz):
            there = drecv[k, pl.ds((PLACE[j] * 2 + dz) * 16, 16), cols_of(h, n)]
            return own(k, j, dz, cols_of(h, n))[...] + there.astype(F32)

        if part == 0:
            ring_send(k, h, n, 0, both(2, 0), fp)
            ring_send(k, h, n, 1, both(2, 1), fm)
            ring_send(k, h, n, 2, both(1, 1), fp)
            rest = ((1, 0),)
        else:
            ring_send(k, h, n, 3, both(3, 0), fm)
            rest = ((3, 1), (0, 0), (0, 1))
        for j, dz in rest:
            own(k, j, dz, cols_of(h, n))[...] = both(j, dz)

    def second(k, h, way):
        n = CHUNKS[k]
        j, dz, dev = ((1, 0, fp), (3, 1, fm))[way]
        value = own(k, j, dz, cols_of(h, n))[...] + ring_wait(k, h, n, way)
        ring_send(k, h, n, 4 + way, value, dev)

    late = []

    def s_wait(k, h):
        at = (k, slice(None) if k != 2 else 0, slice(None), cols_of(h, CHUNKS[k]))

        @pl.when(lax.rem(q + k, 4) != 0)
        def _():
            arrived(srecv.at[at], s_sem.at[k * MAXCH + h])

    def third(k, h):
        n = CHUNKS[k]
        cols = cols_of(h, n)
        parts = [ring_wait(k, h, n, slot) for slot in (2, 3, 4, 5)]
        one = (own(k, 0, 0, cols)[...] + parts[1] + parts[2]).astype(BF16)
        two = (own(k, 0, 1, cols)[...] + parts[0] + parts[3]).astype(BF16)
        s = lax.rem(q + k, 4)
        there = shifted(0, s)
        ssend[k, 0, :, cols] = one
        ssend[k, 1, :, cols] = two
        if k == 2:
            at = (slice(None), cols)
            send(ssend.at[(2, 1, *at)], szrecv.at[at], sz_sem.at[h], (there[0], 1 - z, *there[2:]))
        at = (k, slice(None) if k != 2 else 0, slice(None), cols)
        copy = pltpu.make_async_remote_copy(
            src_ref=ssend.at[at], dst_ref=srecv.at[at],
            send_sem=ss_sem.at[k * MAXCH + h], recv_sem=s_sem.at[k * MAXCH + h],
            device_id=there, device_id_type=MESH,
        )

        @pl.when(s != 0)
        def _():
            copy.start()

        @pl.when(s == 0)
        def _():
            srecv[k, 0, :, cols] = one
            if k != 2:
                srecv[k, 1, :, cols] = two

        late.append((s, copy))

    def zearly():
        for k in (0, 3, 1):
            for h in range(CHUNKS[k]):
                s_wait(k, h)
        for i in range(4):
            cols = cols_of(i, 4)
            mine, other = (
                sum(srecv[k, dz, :, cols].astype(F32) for k in (0, 3, 1)) for dz in (0, 1)
            )
            szown[:, cols] = mine
            zsend[:, cols] = other.astype(BF16)
        send(zsend, zrecv, z_sem, zn)

    def zwait():
        arrived(zrecv, z_sem)

    def final(h):
        cols = cols_of(h, CHUNKS[2])
        at = (slice(None), cols)
        s_wait(2, h)
        arrived(szrecv.at[at], sz_sem.at[h])
        out_ref[at] = (
            szown[at] + zrecv[at].astype(F32) + srecv[2, 0, :, cols].astype(F32) + szrecv[at].astype(F32)
        )

    prepare(3)
    ag(own_ref, 0, 1, 0, 0, sm)
    ag(own_ref, 3, 0, 0, 0, fp)
    prepare(1)
    got(1, 0, 0)
    to_second(1, 0)
    got(0, 1, 0)
    got(0, 0, 1)
    got(0, 3, 0)
    to_second(0, 1)
    prepare(2)
    ag(own_ref, 0, 0, 1, 0, pn)
    got(1, 3, 0)
    ag(slab(0, 0, 0, 1), 1, 0, 0, 1, fm)
    got(0, 2, 0)
    got(0, 1, 1)
    prepare(0)
    got(3, 0, 0)
    partners(0, 0)
    scores(0)
    rq_far(0)
    ag(slab(0, 0, 0, 1), 3, 0, 0, 1, fp)
    rq_near(0)
    to_second(3, 0)
    got(1, 1, 0)
    got(0, 3, 1)
    got(1, 0, 1)
    got(0, 2, 1)
    got(1, 2, 0)
    partners(0, 1)
    to_second(1, 1)
    scores(1)
    rq_far(1)
    partners(1, 0)
    scores(2)
    rq_far(2)
    got(2, 0, 0)
    rq_near(2)
    got(3, 3, 0)
    to_second(2, 0)
    rq_second(0, 0)
    got(2, 0, 1)
    got(1, 1, 1)
    to_second(2, 1)
    got(3, 1, 0)
    rq_second(0, 1)
    got(3, 2, 0)
    got(3, 0, 1)
    rq_near(1)
    rq_second(1, 1)
    rq_second(1, 0)
    rq_second(2, 1)
    got(1, 2, 1)
    to_second(3, 1)
    partners(3, 0)
    scores(6)
    got(2, 3, 0)
    rq_second(2, 0)
    got(2, 1, 1)
    got(2, 3, 1)
    got(1, 3, 1)
    rq_far(6)
    rq_near(6)
    partners(1, 1)
    got(2, 1, 0)
    scores(3)
    got(3, 3, 1)
    rq_far(3)
    got(3, 1, 1)
    rq_third(0)
    got(2, 2, 1)
    partners(2, 1)
    scores(5)
    got(2, 2, 0)
    rq_near(3)
    got(3, 2, 1)
    partners(3, 1)
    partners(2, 0)
    rq_far(5)
    scores(7)
    rq_second(6, 1)
    rq_far(7)
    rq_near(5)
    rq_second(6, 0)
    rq_second(5, 1)
    scores(4)
    rq_second(5, 0)
    rq_far(4)
    rq_third(1)
    rq_second(7, 1)
    rq_near(7)
    rq_third(6)
    rq_near(4)
    rq_second(4, 0)
    rq_third(2)
    rq_second(4, 1)
    rq_second(3, 1)
    rq_second(7, 0)
    rq_second(3, 0)
    rq_third(7)
    rq_third(5)
    rq_third(4)
    rq_third(3)
    peak()
    w_start()
    softmax()
    classes(0, 0, 0)
    classes(0, 1, 0)
    first(0, 0, 0)
    w_wait(3, 1)
    first(0, 1, 0)
    w_wait(1, 0)
    w_wait(1, 1)
    w_wait(3, 0)
    classes(3, 0, 0)
    classes(1, 0, 0)
    second(0, 0, 0)
    classes(1, 0, 1)
    w_wait(1, 2)
    second(0, 0, 1)
    first(3, 0, 0)
    first(1, 0, 0)
    w_wait(3, 3)
    w_wait(3, 2)
    classes(3, 1, 0)
    w_wait(1, 3)
    classes(1, 1, 0)
    first(1, 0, 1)
    classes(1, 1, 1)
    first(3, 1, 0)
    second(3, 0, 1)
    w_wait(2, 1)
    w_wait(2, 0)
    second(3, 0, 0)
    classes(2, 0, 0)
    classes(2, 0, 1)
    first(1, 1, 1)
    second(1, 1, 0)
    third(0, 0)
    second(1, 1, 1)
    second(1, 0, 0)
    first(2, 0, 0)
    first(1, 1, 0)
    w_wait(2, 3)
    w_wait(2, 2)
    classes(2, 1, 0)
    third(3, 0)
    second(1, 0, 1)
    third(1, 1)
    classes(2, 1, 1)
    first(2, 0, 1)
    second(2, 0, 0)
    first(2, 1, 0)
    second(2, 0, 1)
    third(1, 0)
    first(2, 1, 1)
    second(2, 1, 1)
    second(2, 1, 0)
    zearly()
    third(2, 0)
    third(2, 1)
    zwait()
    final(0)
    final(1)

    for s, copy in late:

        @pl.when(s != 0)
        def _():
            copy.wait_send()

    for copy in sends:
        copy.wait_send()


def body(particles, ctf, noise_var, projections, orient_class, class_prior, counts):
    npart, npix = particles.shape
    vmem = pl.BlockSpec(memory_space=pltpu.VMEM)
    smem = pl.BlockSpec(memory_space=pltpu.SMEM)
    hbm = pl.BlockSpec(memory_space=pl.ANY)
    dma = pltpu.SemaphoreType.DMA
    out, norm = pl.pallas_call(
        kernel,
        out_shape=(jax.ShapeDtypeStruct((16, npix), F32), jax.ShapeDtypeStruct((1, npart), F32)),
        in_specs=[hbm, hbm, hbm, hbm, hbm, smem, smem],
        out_specs=(vmem, vmem),
        scratch_shapes=[
            pltpu.VMEM((1, npix), F32),
            pltpu.VMEM((16, npix), BF16),
            pltpu.VMEM((1, 1024), jnp.int32),
            pltpu.VMEM((npart, npix), BF16),
            pltpu.VMEM((npart, npix), BF16),
            pltpu.VMEM((npix, npart), BF16),
            pltpu.VMEM((npix, npart), BF16),
            pltpu.VMEM((1024, npix), BF16),
            pltpu.VMEM((128, npix), BF16),
            pltpu.VMEM((1024, npart), F32),
            pltpu.VMEM((48, 16, npart), F32),
            pltpu.VMEM((256, npart), F32),
            pltpu.VMEM((4, 8, npart), F32),
            pltpu.VMEM((4, 256, npart), BF16),
            pltpu.VMEM((4, 128, npix), F32),
            pltpu.VMEM((4, 128, npix), BF16),
            pltpu.VMEM((4, 128, npix), BF16),
            pltpu.VMEM((24, 16, npix), BF16),
            pltpu.VMEM((24, 16, npix), BF16),
            pltpu.VMEM((4, 2, 16, npix), BF16),
            pltpu.VMEM((4, 2, 16, npix), BF16),
            pltpu.VMEM((16, npix), BF16),
            pltpu.VMEM((16, npix), F32),
            pltpu.VMEM((16, npix), BF16),
            pltpu.VMEM((16, npix), BF16),
            pltpu.VMEM((4, 256, npart), BF16),
            pltpu.VMEM((4, 8, npart), F32),
            dma((11,)), dma((NSEM,)), dma((64,)), dma((48,)), dma((4,)), dma((16,)), dma((8 * MAXCH,)),
            dma((24 * MAXCH,)), dma((4 * MAXCH,)), dma((4 * MAXCH,)), dma((MAXCH,)), dma,
        ],
        compiler_params=pltpu.CompilerParams(
            collective_id=0, has_side_effects=True, vmem_limit_bytes=64 * 1024 * 1024 - 128 * 1024
        ),
    )(particles, ctf, noise_var.reshape(1, npix), projections, orient_class.reshape(1, 1024), class_prior, counts)
    return out, norm.reshape(npart)


def solution(mesh):
    torus = Mesh(
        mesh.devices.reshape(4, 2, 4, 2, mesh.shape["pix"]),
        ("blk_0", "blk_1", "blk_2", "blk_3", "pix"),
    )
    in_specs = (P(BLK, "pix"), P(BLK, "pix"), P("pix"), P(BLK, "pix"), P(), P(), P(BLK))
    out_specs = (P(BLK, "pix"), P(BLK))
    return jax.shard_map(body, mesh=torus, in_specs=in_specs, out_specs=out_specs, check_vma=False)
```

time: 484 us -> 121 us (0.25)
  waiting for transfers between devices: 394 us -> 0 us
  Pallas kernels: 0 us -> 115 us
  blocking collectives: 24 us -> 0 us
  matrix products: 21.2 us -> 0 us
  between operations: 14.5 us -> 1.29 us
  starting transfers between devices: 13.2 us -> 0 us
  local copies, waits for them, and re-layouts: 9.11 us -> 2.92 us
    reduce_scatter x2 -> x0, waiting for transfers between devices: 212 us -> none  [the longest x1 183 us: sum_by_chip_2(): return lax.psum_scatter(tiles, chips, scatter_dimension=0, tiled=True)[0]]
    all_gather x1 -> x0, waiting for transfers between devices: 116 us -> none  [body(): part_rows = lax.all_gather(projections, BLK, axis=0, tiled=True)]
    pallas_call x0 -> x1, Pallas kernels: none -> 115 us  [body(): pl.pallas_call(kernel, out_shape=(jax.ShapeDtypeStruct((16, npix), F32),...]
    all_to_all x3 -> x0, waiting for transfers between devices: 65.7 us -> none  [the longest x1 51 us: summed_on_arrival(): lax.all_to_all(cut_along(value, dim, devices), axis, 0, 0, tiled=True)]
    all_to_all x1 -> x0, blocking collectives: 24 us -> none  [from_everyone(): return lax.all_to_all(copies, axis, split_axis=0, concat_axis=0, tiled=True)]
    dot_general x3 -> x0, matrix products: 21.2 us -> none  [the longest x1 9.56 us: body(): lax.dot_general(weighted, part_rows, (((1,), (1,)), ((), ())), preferred_...]
    all_to_all x3 -> x0, starting transfers between devices: 13.1 us -> none  [the longest x1 6.56 us: summed_on_arrival(): lax.all_to_all(cut_along(value, dim, devices), axis, 0, 0, tiled=True)]
    transpose x1 -> x0, local copies, waits for them, and re-layouts: 6.03 us -> none  [sum_by_chip_2(): tiles = tiles.reshape(*sizes, *inside).swapaxes(0, 1).reshape(-1, *inside)]
  transfers between devices with their start and end apart: 6 -> 0, of which waited for: 6 -> 0; matrix products, arithmetic and copies ran while one was open for 0% -> 0% of each run, Pallas kernels for 0% -> 0%
where the time goes in v2:
time: 121 us; the launch traced here: 119 us
  Pallas kernels  115 us (95%)
  local copies, waits for them, and re-layouts  2.92 us (2%)
  between operations  1.29 us (1%)
    pallas_call x1, Pallas kernels, body(): pl.pallas_call(kernel, out_shape=(jax.ShapeDtypeStruct((16, npix), F32),...  115 us
    unnamed x2, local copies, waits for them, and re-layouts  2.92 us

profile of v2, /device:TPU:8, one launch (start us, length us, event | category | flops | bytes accessed | tf_op | source)
XLA Modules:
  0.0 119.0 jit_solution(5890951683520601867)
XLA Ops:
  1.3 114.8 %shard_map.86 = (f32[16,4096]{1,0:T(8,128)}, f32[1,512]{1,0:T(1,128)}) custom-call(bf16[512,4096]{1,0:T(8,128)(2,1)} %part_hbm.1, bf16[512,4096]{1,0:T(8,128)(2,1)} %ctf_hbm.1, f32[1,4096]{1,0:T(1,128)} %bitcast.3, bf16[16,4096]{1,0:T(8,128)(2,1)} %own_hbm.1, s32[1,1024]{1,0:T(1,128)} %bitcast.4, f32[5]{0:T(128)} %cp_ref.1, s32[1]{0:T(128)S(6)} %copy.11.cnt_ref), custom_call_target="tpu_custom_call" | custom-call | tf_op jit(solution)/shard_map/pallas_call | solution.py:546
  116.1 1.7 %copy.12 = f32[16,4096]{1,0:T(8,128)} copy(f32[16,4096]{1,0:T(8,128)} %get-tuple-element.8) | data formatting | bytes 524288
  117.7 1.2 %copy.13 = f32[512]{0:T(512)} copy(f32[512]{0:T(512)} %bitcast.5) | data formatting | bytes 4096

commit v3 on v2

--- a/solution.py
+++ b/solution.py
@@ -80,9 +80,6 @@
             cp.start()
             loads.append(cp)
 
-    small[0].wait()
-    pl.semaphore_wait(barrier, len(peers))
-
     def slab_no(f, s, k, dz):
         return (((f % 4) * 2 + dz) * 4 + s % 4) * 2 + k
 
@@ -102,13 +99,9 @@
         ag(slab(f, 0, 0, dz), f, 3, 0, dz, sp)
         ag(slab(f, 0, 0, dz), f, 1, 0, dz, sm)
 
-    ag(own_ref, 0, 0, 0, 1, zn)
-    ag(own_ref, 1, 0, 0, 0, fm)
-    ag(own_ref, 0, 3, 0, 0, sp)
-    slab(0, 0, 0, 0)[...] = own_ref[...]
-
     small[1].wait()
     small[2].wait()
+
     def prepare(i):
         loads[2 * i].wait()
         loads[2 * i + 1].wait()
@@ -123,6 +116,15 @@
             wgt[at, cols] = weighted
             wgt_t[cols, at] = weighted.T
             quad_t[cols, at] = (0.5 * wide * wide * inv).astype(BF16).T
+
+    prepare(0)
+    small[0].wait()
+    pl.semaphore_wait(barrier, len(peers))
+
+    ag(own_ref, 0, 0, 0, 1, zn)
+    ag(own_ref, 1, 0, 0, 0, fm)
+    ag(own_ref, 0, 3, 0, 0, sp)
+    slab(0, 0, 0, 0)[...] = own_ref[...]
 
     lane = lax.broadcasted_iota(jnp.int32, (1, 1024), 1)
     prior_row = jnp.zeros((1, 1024), F32)
@@ -378,7 +380,6 @@
     ag(slab(0, 0, 0, 1), 1, 0, 0, 1, fm)
     got(0, 2, 0)
     got(0, 1, 1)
-    prepare(0)
     got(3, 0, 0)
     partners(0, 0)
     scores(0)

time: 121 us -> 120 us (level); the launches traced: 119 us -> 120 us
  no operation moved by 1% of the time
where the time goes in v3:
time: 120 us
  Pallas kernels  116 us (97%)
  local copies, waits for them, and re-layouts  2.92 us (2%)
  between operations  1.29 us (1%)
    pallas_call x1, Pallas kernels, body(): pl.pallas_call(kernel, out_shape=(jax.ShapeDtypeStruct((16, npix), F32),...  116 us
    unnamed x2, local copies, waits for them, and re-layouts  2.92 us

profile of v3, /device:TPU:8, one launch (start us, length us, event | category | flops | bytes accessed | tf_op | source)
XLA Modules:
  0.0 120.1 jit_solution(12298643881560663238)
XLA Ops:
  1.3 115.9 %shard_map.86 = (f32[16,4096]{1,0:T(8,128)}, f32[1,512]{1,0:T(1,128)}) custom-call(bf16[512,4096]{1,0:T(8,128)(2,1)} %part_hbm.1, bf16[512,4096]{1,0:T(8,128)(2,1)} %ctf_hbm.1, f32[1,4096]{1,0:T(1,128)} %bitcast.3, bf16[16,4096]{1,0:T(8,128)(2,1)} %own_hbm.1, s32[1,1024]{1,0:T(1,128)} %bitcast.4, f32[5]{0:T(128)} %cp_ref.1, s32[1]{0:T(128)S(6)} %copy.11.cnt_ref), custom_call_target="tpu_custom_call" | custom-call | tf_op jit(solution)/shard_map/pallas_call | solution.py:547
  117.2 1.7 %copy.12 = f32[16,4096]{1,0:T(8,128)} copy(f32[16,4096]{1,0:T(8,128)} %get-tuple-element.8) | data formatting | bytes 524288
  118.8 1.2 %copy.13 = f32[512]{0:T(512)} copy(f32[512]{0:T(512)} %bitcast.5) | data formatting | bytes 4096
